TPU v7x, 32 devices: a whole 2x2x4 slice. The times are simulated.
32 devices in a mesh: beam: 8 (over z, y), mp: 4 (over x, core).
Axes of the slice: x: 2, y: 2, z: 4, core: 2. Of those that a mesh axis runs over, the one named last changes fastest.
Arguments:
- token_ids: int32 [512], P('beam'), may hold values from 0 to 128255
- parents: int32 [64, 8, 1], P('beam'), may hold values from 0 to 7; in each aligned block of 512 rows (0 to 511, 512 to 1023, ..., all dimensions but the last counted through in order) at most 192 rows name the same one
- embedding: bfloat16 [128256, 8192], P('mp', 'beam'), may hold values from -6 to 6
- norm_gain: bfloat16 [8192], P('beam'), may hold values from 0.099609375 to 1.8984375
- query_weight: bfloat16 [8192, 8192], P('beam', 'mp'), may hold values from -0.0625 to 0.0625
- key_weight: bfloat16 [8192, 1024], P('beam', 'mp'), may hold values from -0.0625 to 0.0625
- value_weight: bfloat16 [8192, 1024], P('beam', 'mp'), may hold values from -0.0625 to 0.0625
- output_weight: bfloat16 [8192, 8192], P('mp', 'beam'), may hold values from -0.0625 to 0.0625
- cache_keys: bfloat16 [512, 512, 1024], P('beam', None, 'mp'), may hold values from -30 to 30
- cache_values: bfloat16 [512, 512, 1024], P('beam', None, 'mp'), may hold values from -32 to 32
Outputs:
- attention_out: bfloat16 [512, 8192], P('mp', 'beam')
- new_keys: bfloat16 [512, 1024], P('beam', 'mp')
- new_values: bfloat16 [512, 1024], P('beam', 'mp')
Inputs may be any that keep to these rules, and one draw needn't show every extreme that they name: parents lie in 0 to 7. Split the requests into aligned blocks of 64 requests; among the new beams of one block, no parent index is named more than 192 times, and in some blocks one is named exactly 192 times.
All inputs are finite; a program needn't handle non-finite values.
Results may differ from a plain program's by a relative error of at most 0.0071.
The roundings to bfloat16 on the way count: a program that leaves them out, or rounds other values in their place, can miss the bound.
Values may be sent and summed in bfloat16 or wider, within the bound.
No kernel may reach another device: no remote copies, remote signals or barrier semaphores. Data moves between devices by JAX's collectives and lax.ppermute only.
A program may use at most 320 MiB of HBM per device.

v0:
```python
import jax
import jax.numpy as jnp
from jax import lax
from jax.sharding import PartitionSpec as P

D = 8192
HEAD_DIM = 128
LEN = 512
REQS = 64
BEAMS = 8
LOAD = 3
epsilon = 1e-05
rope_base = 500000.0


def apply_rotary(tensor):
    half_dim = HEAD_DIM // 2
    frequency = rope_base ** (-(jnp.arange(half_dim, dtype=jnp.float32) * 2.0 / HEAD_DIM))
    angles = LEN * frequency
    cosine_table = jnp.cos(angles)
    sine_part = jnp.sin(angles)
    front_half = tensor[..., :half_dim]
    back_half = tensor[..., half_dim:]
    return jnp.concatenate(
        [
            front_half * cosine_table - back_half * sine_part,
            back_half * cosine_table + front_half * sine_part,
        ],
        axis=-1,
    )


def finish(query_total, key_total, value_total, square_total):
    inverse = (1.0 / jnp.sqrt(square_total / D + epsilon))[:, None]
    row_count = query_total.shape[0]
    query_matrix = (
        apply_rotary((query_total * inverse).reshape(row_count, -1, HEAD_DIM))
        .astype(jnp.bfloat16)
        .reshape(row_count, -1)
    )
    fresh_keys = (
        apply_rotary((key_total * inverse).reshape(row_count, -1, HEAD_DIM))
        .astype(jnp.bfloat16)
        .reshape(row_count, -1)
    )
    fresh_values = (value_total * inverse).astype(jnp.bfloat16)
    return (query_matrix, fresh_keys, fresh_values)


def attend(query_matrix, self_key_rows, own_values, slot_keys, slot_values):
    scale_factor = HEAD_DIM ** (-0.5)
    scores = (
        jnp.einsum("bkgd,blkd->bkgl", query_matrix, slot_keys, preferred_element_type=jnp.float32)
        * scale_factor
    )
    own_score = (
        jnp.einsum("nlem,nlm->nle", query_matrix, self_key_rows, preferred_element_type=jnp.float32)
        * scale_factor
    )
    ceiling = jnp.maximum(jnp.max(scores, axis=-1), own_score)
    weights = jnp.exp(scores - ceiling[..., None])
    own_weight = jnp.exp(own_score - ceiling)
    softmax_divisor = jnp.sum(weights, axis=-1) + own_weight
    attention_weights = (weights / softmax_divisor[..., None]).astype(jnp.bfloat16)
    own_share = (own_weight / softmax_divisor).astype(jnp.bfloat16)
    mixture = jnp.einsum(
        "bkgl,blkd->bkgd", attention_weights, slot_values, preferred_element_type=jnp.float32
    )
    mixture = (
        mixture
        + own_share.astype(jnp.float32)[..., None] * own_values.astype(jnp.float32)[:, :, None, :]
    )
    return mixture.astype(jnp.bfloat16)


def body(
    token_ids,
    parents,
    embedding,
    norm_gain,
    query_weight,
    key_weight,
    value_weight,
    output_weight,
    cache_keys,
    cache_values,
):
    all_ids, all_parents = (
        lax.all_gather(token_ids, "beam", axis=0, tiled=True),
        lax.all_gather(parents, "beam", axis=0, tiled=True),
    )
    vocab_local = embedding.shape[0]
    vocab_start = lax.axis_index("mp") * vocab_local
    one_hot = (
        all_ids[:, None] == vocab_start + lax.broadcasted_iota(jnp.int32, (1, vocab_local), 1)
    ).astype(jnp.bfloat16)
    looked_up = jnp.dot(one_hot, embedding, preferred_element_type=jnp.float32)
    embedded = lax.psum(looked_up.astype(jnp.bfloat16), "mp")
    widened = embedded.astype(jnp.float32)
    squares = jnp.sum(widened * widened, axis=1)
    scaled = (widened * norm_gain.astype(jnp.float32)[None, :]).astype(jnp.bfloat16)
    query_portion = jnp.dot(scaled, query_weight, preferred_element_type=jnp.float32)
    key_part = jnp.dot(scaled, key_weight, preferred_element_type=jnp.float32)
    value_part = jnp.dot(scaled, value_weight, preferred_element_type=jnp.float32)
    row_local = cache_keys.shape[0]
    first_row = lax.axis_index("beam") * row_local
    query_total, key_total, value_total, square_total = lax.psum(
        (query_portion, key_part, value_part, squares), "beam"
    )
    query_matrix, fresh_keys, fresh_values = finish(
        query_total, key_total, value_total, square_total
    )
    keys_out = lax.dynamic_slice_in_dim(fresh_keys, first_row, row_local, 0)
    values_out = lax.dynamic_slice_in_dim(fresh_values, first_row, row_local, 0)
    key_heads = key_weight.shape[1] // HEAD_DIM
    query_heads = query_weight.shape[1] // HEAD_DIM
    groups = query_heads // key_heads
    query_width = query_heads * HEAD_DIM
    key_width = key_heads * HEAD_DIM
    parent_beam = first_row // REQS
    request_start = first_row % REQS
    offspring_query_rows = lax.dynamic_slice_in_dim(
        query_matrix.reshape(BEAMS, REQS, query_width), request_start, row_local, 1
    )
    child_keys = lax.dynamic_slice_in_dim(
        fresh_keys.reshape(BEAMS, REQS, key_width), request_start, row_local, 1
    )
    child_values = lax.dynamic_slice_in_dim(
        fresh_values.reshape(BEAMS, REQS, key_width), request_start, row_local, 1
    )
    parent_block = lax.dynamic_slice_in_dim(all_parents[:, :, 0], request_start, row_local, 0)
    matches = jnp.transpose(parent_block) == parent_beam
    slot_keys = cache_keys.reshape(row_local, LEN, key_heads, HEAD_DIM)
    slot_values = cache_values.reshape(row_local, LEN, key_heads, HEAD_DIM)
    count_all = BEAMS * row_local
    is_child = matches.reshape(count_all).astype(jnp.int32)
    position = jnp.cumsum(is_child) - 1
    capacity = LOAD * row_local
    select_ones = (
        (position[None, :] == lax.broadcasted_iota(jnp.int32, (capacity, 1), 0))
        & (is_child[None, :] == 1)
    ).astype(jnp.int32)
    selector = select_ones.astype(jnp.bfloat16)
    slot_index = jnp.sum(
        select_ones * (lax.broadcasted_iota(jnp.int32, (1, count_all), 1) % row_local), axis=1
    )
    packed = jnp.concatenate(
        [
            offspring_query_rows.reshape(count_all, query_width),
            child_keys.reshape(count_all, key_width),
            child_values.reshape(count_all, key_width),
        ],
        axis=1,
    )
    picked = jnp.dot(selector, packed, preferred_element_type=jnp.float32).astype(jnp.bfloat16)
    mixture = attend(
        picked[:, :query_width].reshape(capacity, key_heads, groups, HEAD_DIM),
        picked[:, query_width : query_width + key_width].reshape(capacity, key_heads, HEAD_DIM),
        picked[:, query_width + key_width :].reshape(capacity, key_heads, HEAD_DIM),
        slot_keys[slot_index],
        slot_values[slot_index],
    )
    masked_rows = (
        jnp.dot(
            jnp.transpose(selector),
            mixture.reshape(capacity, query_width),
            preferred_element_type=jnp.float32,
        )
        .astype(jnp.bfloat16)
        .reshape(BEAMS, row_local, query_width)
    )
    positioned_rows = lax.dynamic_update_slice_in_dim(
        jnp.zeros((BEAMS, REQS, query_width), jnp.float32),
        masked_rows.astype(jnp.float32),
        request_start,
        1,
    )
    attended = lax.psum(
        positioned_rows.reshape(BEAMS * REQS, query_width).astype(jnp.bfloat16), "beam"
    )
    attention_out = lax.psum_scatter(
        jnp.dot(attended, output_weight, preferred_element_type=jnp.float32),
        "mp",
        scatter_dimension=0,
        tiled=True,
    ).astype(jnp.bfloat16)
    return (attention_out, keys_out, values_out)


def solution(mesh):
    return jax.shard_map(
        body,
        mesh=mesh,
        in_specs=(
            P("beam"),
            P("beam", None, None),
            P("mp", "beam"),
            P("beam"),
            P("beam", "mp"),
            P("beam", "mp"),
            P("beam", "mp"),
            P("mp", "beam"),
            P("beam", None, "mp"),
            P("beam", None, "mp"),
        ),
        out_specs=(P("mp", "beam"), P("beam", "mp"), P("beam", "mp")),
        check_vma=False,
    )
```

profile of v0, /device:TPU:0, one launch (start us, length us, event | category | flops | bytes accessed | tf_op | source)
XLA Modules:
  0.0 505.2 jit_solution(15561030509055637348)
XLA Ops:
  7.3 1.3 dynamic-slice
  9.2 0.9 dynamic-update-slice
  10.1 13.1 %all-reduce = s32[512]{0:T(512)S(1)} all-reduce(s32[512]{0:T(512)S(1)} %dynamic-update-slice), channel_id=1, replica_groups=mesh['beam'=8,'mp'=4] {'beam'}, use_global_device_ids=true, to_apply=%add | all-reduce | flops 512 | bytes 4096
  23.2 40.7 %fusion.16 = bf16[512,1024]{1,0:T(8,128)(2,1)} fusion(bf16[32064,1024]{1,0:T(8,128)(2,1)} %param.12, s32[32064]{0:T(1024)S(1)} %iota_add_fusion, s32[512]{0:T(512)S(1)} %all-reduce), kind=kOutput, calls=%fused_computation.31 | convolution fusion | flops 33638481920 | bytes 66845952 | tf_op jit(solution)/shard_map/dot_general | solution.py:97
  64.0 34.6 %all-reduce.6.cloned.1.call-done = bf16[512,1024]{1,0:T(8,128)(2,1)} async-done(((bf16[512,1024]{1,0:T(8,128)(2,1)}), bf16[512,1024]{1,0:T(8,128)(2,1)}) %all-reduce.6.cloned.1.call-update) | async-done | bytes 1048592 | tf_op jit(solution)/shard_map/psum | solution.py:98
  98.6 6.9 %fusion.23 = f32[512,2048]{1,0:T(8,128)} fusion(bf16[1024,2048]{1,0:T(8,128)(2,1)} %param.14, bf16[512,1024]{1,0:T(8,128)(2,1)} %all-reduce.6.cloned.1.call-done, f32[1024]{0:T(1024)S(1)} %convert_element_type.98), kind=kOutput, calls=%fused_computation.34 | convolution fusion | flops 2149056512 | bytes 9441280 | tf_op jit(solution)/shard_map/dot_general | solution.py:102
  105.5 1.2 fusion.19
  106.7 1.3 fusion.21
  108.1 31.9 %all_gather.6 = s32[64,8,1]{1,2,0:T(1,128)S(1)} all-gather(s32[8,8,1]{1,2,0:T(1,128)S(1)} %copy-done.3), channel_id=1, replica_groups=mesh['beam'=8,'mp'=4] {'beam'}, dimensions={0}, use_global_device_ids=true | all-gather | bytes 2304 | tf_op jit(solution)/shard_map/all_gather | solution.py:90
  140.7 22.5 %copy.43 = bf16[64,512,256]{1,2,0:T(8,128)(2,1)} copy(bf16[64,512,256]{2,1,0:T(8,128)(2,1)} %param.18) | data formatting | bytes 33554432 | tf_op args[8]
  163.2 22.2 %copy.44 = bf16[64,512,2,128]{3,1,2,0:T(8,128)(2,1)} copy(bf16[64,512,2,128]{1,3,2,0:T(8,128)(2,1)} %bitcast.61) | data formatting | bytes 33554432 | tf_op jit(solution)/shard_map/reshape | solution.py:133
  185.4 22.5 %copy.49 = bf16[64,512,256]{1,2,0:T(8,128)(2,1)} copy(bf16[64,512,256]{2,1,0:T(8,128)(2,1)} %param.19) | data formatting | bytes 33554432 | tf_op args[9]
  208.0 22.4 %copy.50 = bf16[64,512,2,128]{3,1,2,0:T(8,128)(2,1)} copy(bf16[64,512,2,128]{1,3,2,0:T(8,128)(2,1)} %bitcast.62) | data formatting | bytes 33554432 | tf_op jit(solution)/shard_map/reshape | solution.py:134
  230.8 25.1 %gather_fusion = bf16[192,512,2,128]{3,1,2,0:T(8,128)(2,1)} fusion(bf16[64,512,2,128]{3,1,2,0:T(8,128)(2,1)} %copy.44, s32[1024]{0:T(1024)S(1)} %pad_clamp_fusion), kind=kCustom, calls=%fused_computation | custom fusion | bytes 100664064 | tf_op jit(solution)/shard_map/gather | solution.py:160
  255.9 23.7 %gather_fusion.1 = bf16[192,512,2,128]{3,1,2,0:T(8,128)(2,1)} fusion(bf16[64,512,2,128]{3,1,2,0:T(8,128)(2,1)} %copy.50, s32[1024]{0:T(1024)S(1)} %pad_clamp_fusion), kind=kCustom, calls=%fused_computation.1 | custom fusion | bytes 100664064 | tf_op jit(solution)/shard_map/gather | solution.py:161
  280.0 21.2 %psum.44 = f32[512]{0:T(512)S(1)} all-reduce(f32[512]{0:T(512)S(1)} %fusion.15), channel_id=1, replica_groups=mesh['beam'=8,'mp'=4] {'beam'}, use_global_device_ids=true, to_apply=%region_5.0 | all-reduce | flops 512 | bytes 4096 | tf_op jit(solution)/shard_map/psum | solution.py:107
  301.2 1.3 broadcast_multiply_fusion
  303.0 2.5 multiply_bitcast_fusion
  305.6 0.9 copy.55
  306.5 1.4 subtract_convert_fusion
  307.9 1.2 pad_maximum_fusion
  309.6 0.7 convolution_convert_fusion
  311.2 22.1 %multiply_reduce_fusion = (f32[192,2,8]{2,1,0:T(2,128)S(1)}, f32[192,2,8,512]{3,2,1,0:T(8,128)}) fusion(bf16[192,2,8,128]{3,2,1,0:T(8,128)(2,1)S(1)} %bitcast.66, bf16[192,512,2,128]{3,1,2,0:T(8,128)(2,1)} %gather_fusion), kind=kOutput, calls=%fused_computation.8 | convolution fusion | flops 405795840 | bytes 57421824 | tf_op jit(solution)/shard_map/bkgd,blkd->bkgl/dot_general | solution.py:53
  333.7 3.8 fusion.4
  338.0 20.1 %add_convert_fusion.1 = bf16[192,2,8,128]{3,2,1,0:T(8,128)(2,1)S(1)} fusion(bf16[192,512,2,128]{3,1,2,0:T(8,128)(2,1)} %gather_fusion.1, f32[192,2,8,512]{3,2,1,0:T(8,128)} %get-tuple-element.19, f32[192,2,8]{2,1,0:T(2,128)S(1)} %copy.48, f32[192,2,8]{2,1,0:T(2,128)S(1)} %copy.46, f32[192,2,128]{2,1,0:T(2,128)S(1)} %reshape.154, f32[192,2,8]{2,1,0:T(2,128)S(1)} %copy.51), kind=kOutput, calls=%fused_computation.30 | convolution fusion | flops 410124288 | bytes 57643008 | tf_op jit(solution)/shard_map/bkgl,blkd->bkgd/dot_general | solution.py:66
  358.1 2.0 convolution_convert_fusion.1
  360.3 99.5 %all-reduce.8.cloned.1.call-done = bf16[512,2048]{1,0:T(8,128)(2,1)} async-done(((bf16[512,2048]{1,0:T(8,128)(2,1)}), bf16[512,2048]{1,0:T(8,128)(2,1)}) %all-reduce.8.cloned.1.call-update) | async-done | bytes 2097168 | tf_op jit(solution)/shard_map/psum | solution.py:178
  459.7 6.5 %fusion.44 = f32[512,1024]{1,0:T(8,128)} fusion(bf16[512,2048]{1,0:T(8,128)(2,1)} %all-reduce.8.cloned.1.call-done, bf16[2048,1024]{1,0:T(8,128)(2,1)} %param.17), kind=kOutput, calls=%fused_computation.81 | convolution fusion | flops 2147483648 | bytes 8388608 | tf_op jit(solution)/shard_map/dot_general | solution.py:182
  466.3 0.6 constant_dynamic-slice_fusion.1
  466.9 0.6 constant_dynamic-slice_fusion
  467.5 29.4 %reduce-scatter.2.cloned.1.call-done = f32[128,1024]{1,0:T(8,128)} async-done(((f32[512,1024]{1,0:T(8,128)}), f32[128,1024]{1,0:T(8,128)}) %reduce-scatter.2.cloned.1.call-update) | async-done | bytes 524304 | tf_op jit(solution)/shard_map/reduce_scatter | solution.py:181
  496.9 1.8 convert_element_type.111
  (60 shorter events, 4.4 us)
Async XLA Ops:
  7.2 98.3 %copy-start = (bf16[1024,256]{1,0:T(8,128)(2,1)S(1)}, bf16[1024,256]{1,0:T(8,128)(2,1)}, u32[]{:S(2)}) copy-start(bf16[1024,256]{1,0:T(8,128)(2,1)} %param.16) | copy-start | bytes 1572868
  7.2 91.4 %all-reduce.6.cloned.1.call-start = ((), (), s32[]{:S(2)}) async-start(), calls=%async_computation.1 | async-start | bytes 2097152 | tf_op jit(solution)/shard_map/psum | solution.py:98
  23.2 40.8 %copy-start.4 = (bf16[1024]{0:T(1024)(128)(2,1)S(1)}, bf16[1024]{0:T(1024)(128)(2,1)}, u32[]{:S(2)}) copy-start(bf16[1024]{0:T(1024)(128)(2,1)} %param.13) | copy-start | bytes 6148
  63.9 237.3 %all-reduce.10.cloned.1.call-start = ((), (), s32[]{:S(2)}) async-start(), calls=%async_computation.4 | async-start | bytes 10485760 | tf_op jit(solution)/shard_map/psum | solution.py:107
  64.0 42.7 %copy-start.5 = (bf16[1024,256]{1,0:T(8,128)(2,1)S(1)}, bf16[1024,256]{1,0:T(8,128)(2,1)}, u32[]{:S(2)}) copy-start(bf16[1024,256]{1,0:T(8,128)(2,1)} %param.15) | copy-start | bytes 1572868
  98.6 6.9 %copy-start.2 = (bf16[512,1024]{1,0:T(8,128)(2,1)S(1)}, bf16[512,1024]{1,0:T(8,128)(2,1)}, u32[]{:S(2)}) copy-start(bf16[512,1024]{1,0:T(8,128)(2,1)} %all-reduce.6.cloned.1.call-done) | copy-start | bytes 3145732
  106.7 1.4 copy-start.3
  108.0 351.7 %all-reduce.8.cloned.1.call-start = ((), (), s32[]{:S(2)}) async-start(), calls=%async_computation.2 | async-start | bytes 4194304 | tf_op jit(solution)/shard_map/psum | solution.py:178
  360.2 136.7 %reduce-scatter.2.cloned.1.call-start = ((), (), s32[]{:S(2)}) async-start(), calls=%async_computation.3 | async-start | bytes 2621440 | tf_op jit(solution)/shard_map/reduce_scatter | solution.py:181
  459.7 38.9 %copy-start.1 = (bf16[1024,256]{1,0:T(8,128)(2,1)S(1)}, bf16[1024,256]{1,0:T(8,128)(2,1)}, u32[]{:S(2)}) copy-start(bf16[1024,256]{1,0:T(8,128)(2,1)} %param.16) | copy-start | bytes 1572868
Sparse Core Ops, SparseCore 0:
  64.0 34.4 all-reduce.5
  108.1 184.6 all-reduce.9
  360.3 99.3 all-reduce.7
  466.4 30.4 reduce-scatter.1
where the time goes:
time: 508 us; the launch traced here: 505 us
  waiting for transfers between devices  163 us (32%)
  local copies, waits for them, and re-layouts  145 us (29%)
  matrix products  102 us (20%)
  blocking collectives  66.2 us (13%)
  between operations  14.7 us (3%)
  other arithmetic  13.1 us (3%)
    psum x1, waiting for transfers between devices, body(): lax.psum(positioned_rows.reshape(BEAMS * REQS, query_width).astype(jnp.bf...  99.5 us
    unnamed x21, local copies, waits for them, and re-layouts  49 us
    dot_general x1, matrix products, body(): looked_up = jnp.dot(one_hot, embedding, preferred_element_type=jnp.float32)  40.7 us
    psum x1, waiting for transfers between devices, body(): embedded = lax.psum(looked_up.astype(jnp.bfloat16), 'mp')  34.6 us
    all_gather x1, blocking collectives, body(): lax.all_gather(parents, 'beam', axis=0, tiled=True)  31.9 us
    reduce_scatter x1, waiting for transfers between devices, body(): lax.psum_scatter(jnp.dot(attended, output_weight, preferred_element_type=...  29.4 us
    gather x1, local copies, waits for them, and re-layouts, body(): slot_keys[slot_index]  25.1 us
    gather x1, local copies, waits for them, and re-layouts, body(): slot_values[slot_index]  23.7 us
  transfers between devices with their start and end apart: 4, of which 3 were waited for; matrix products, arithmetic and copies ran while one was open for 28% of the time, Pallas kernels for 0%

commit v1 on v0

--- a/solution.py
+++ b/solution.py
@@ -11,6 +11,7 @@
 LOAD = 3
 epsilon = 1e-05
 rope_base = 500000.0
+boxes_unite = lambda piece_in, axis_id: jnp.sum(lax.all_gather(piece_in, axis_id), axis=0)
 
 
 def apply_rotary(tensor):
@@ -175,7 +176,7 @@
         request_start,
         1,
     )
-    attended = lax.psum(
+    attended = boxes_unite(
         positioned_rows.reshape(BEAMS * REQS, query_width).astype(jnp.bfloat16), "beam"
     )
     attention_out = lax.psum_scatter(

time: 508 us -> 641 us (1.26)
  waiting for transfers between devices: 163 us -> 287 us
  other arithmetic: 13.1 us -> 22.6 us
    all_gather x0 -> x1, waiting for transfers between devices: none -> 224 us  [lax.all_gather(piece_in, axis_id)]
    psum x1 -> x0, waiting for transfers between devices: 99.5 us -> none  [body(): lax.psum(positioned_rows.reshape(BEAMS * REQS, query_width).astype(jnp.bf...]
    reduce_sum x0 -> x1, other arithmetic: none -> 9.45 us  [jnp.sum(lax.all_gather(piece_in, axis_id), axis=0)]
  transfers between devices with their start and end apart: 4 -> 4, of which waited for: 3 -> 3; matrix products, arithmetic and copies ran while one was open for 28% -> 22% of each run, Pallas kernels for 0% -> 0%
where the time goes in v1:
time: 641 us; the launch traced here: 638 us
  waiting for transfers between devices  287 us (45%)
  local copies, waits for them, and re-layouts  145 us (23%)
  matrix products  102 us (16%)
  blocking collectives  66.2 us (10%)
  other arithmetic  22.6 us (4%)
  between operations  14.7 us (2%)
    all_gather x1, waiting for transfers between devices, lax.all_gather(piece_in, axis_id)  224 us
    unnamed x21, local copies, waits for them, and re-layouts  49 us
    dot_general x1, matrix products, body(): looked_up = jnp.dot(one_hot, embedding, preferred_element_type=jnp.float32)  40.7 us
    psum x1, waiting for transfers between devices, body(): embedded = lax.psum(looked_up.astype(jnp.bfloat16), 'mp')  34.6 us
    all_gather x1, blocking collectives, body(): lax.all_gather(parents, 'beam', axis=0, tiled=True)  31.9 us
    reduce_scatter x1, waiting for transfers between devices, body(): lax.psum_scatter(jnp.dot(attended, output_weight, preferred_element_type=...  28.2 us
    gather x1, local copies, waits for them, and re-layouts, body(): slot_keys[slot_index]  25.1 us
    gather x1, local copies, waits for them, and re-layouts, body(): slot_values[slot_index]  23.7 us
  transfers between devices with their start and end apart: 4, of which 3 were waited for; matrix products, arithmetic and copies ran while one was open for 22% of the time, Pallas kernels for 0%

profile of v1, /device:TPU:0, one launch (start us, length us, event | category | flops | bytes accessed | tf_op | source)
XLA Modules:
  0.0 638.0 jit_solution(7929236506106682877)
XLA Ops:
  7.3 1.3 dynamic-slice
  9.2 0.9 dynamic-update-slice
  10.1 13.1 %all-reduce = s32[512]{0:T(512)S(1)} all-reduce(s32[512]{0:T(512)S(1)} %dynamic-update-slice), channel_id=1, replica_groups=mesh['beam'=8,'mp'=4] {'beam'}, use_global_device_ids=true, to_apply=%add | all-reduce | flops 512 | bytes 4096
  23.2 40.7 %fusion.16 = bf16[512,1024]{1,0:T(8,128)(2,1)} fusion(bf16[32064,1024]{1,0:T(8,128)(2,1)} %param.12, s32[32064]{0:T(1024)S(1)} %iota_add_fusion, s32[512]{0:T(512)S(1)} %all-reduce), kind=kOutput, calls=%fused_computation.31 | convolution fusion | flops 33638481920 | bytes 66845952 | tf_op jit(solution)/shard_map/dot_general | solution.py:98
  64.0 34.6 %all-reduce.5.cloned.1.call-done = bf16[512,1024]{1,0:T(8,128)(2,1)} async-done(((bf16[512,1024]{1,0:T(8,128)(2,1)}), bf16[512,1024]{1,0:T(8,128)(2,1)}) %all-reduce.5.cloned.1.call-update) | async-done | bytes 1048592 | tf_op jit(solution)/shard_map/psum | solution.py:99
  98.6 6.9 %fusion.23 = f32[512,2048]{1,0:T(8,128)} fusion(bf16[1024,2048]{1,0:T(8,128)(2,1)} %param.14, bf16[512,1024]{1,0:T(8,128)(2,1)} %all-reduce.5.cloned.1.call-done, f32[1024]{0:T(1024)S(1)} %convert_element_type.100), kind=kOutput, calls=%fused_computation.34 | convolution fusion | flops 2149056512 | bytes 9441280 | tf_op jit(solution)/shard_map/dot_general | solution.py:103
  105.5 1.2 fusion.19
  106.7 1.3 fusion.21
  108.1 31.9 %all_gather.12 = s32[64,8,1]{1,2,0:T(1,128)S(1)} all-gather(s32[8,8,1]{1,2,0:T(1,128)S(1)} %copy-done.3), channel_id=1, replica_groups=mesh['beam'=8,'mp'=4] {'beam'}, dimensions={0}, use_global_device_ids=true | all-gather | bytes 2304 | tf_op jit(solution)/shard_map/all_gather | solution.py:91
  140.7 22.5 %copy.43 = bf16[64,512,256]{1,2,0:T(8,128)(2,1)} copy(bf16[64,512,256]{2,1,0:T(8,128)(2,1)} %param.18) | data formatting | bytes 33554432 | tf_op args[8]
  163.2 22.2 %copy.44 = bf16[64,512,2,128]{3,1,2,0:T(8,128)(2,1)} copy(bf16[64,512,2,128]{1,3,2,0:T(8,128)(2,1)} %bitcast.62) | data formatting | bytes 33554432 | tf_op jit(solution)/shard_map/reshape | solution.py:134
  185.4 22.5 %copy.49 = bf16[64,512,256]{1,2,0:T(8,128)(2,1)} copy(bf16[64,512,256]{2,1,0:T(8,128)(2,1)} %param.19) | data formatting | bytes 33554432 | tf_op args[9]
  208.0 22.4 %copy.50 = bf16[64,512,2,128]{3,1,2,0:T(8,128)(2,1)} copy(bf16[64,512,2,128]{1,3,2,0:T(8,128)(2,1)} %bitcast.63) | data formatting | bytes 33554432 | tf_op jit(solution)/shard_map/reshape | solution.py:135
  230.8 25.1 %gather_fusion = bf16[192,512,2,128]{3,1,2,0:T(8,128)(2,1)} fusion(bf16[64,512,2,128]{3,1,2,0:T(8,128)(2,1)} %copy.44, s32[1024]{0:T(1024)S(1)} %pad_clamp_fusion), kind=kCustom, calls=%fused_computation | custom fusion | bytes 100664064 | tf_op jit(solution)/shard_map/gather | solution.py:161
  255.9 23.7 %gather_fusion.1 = bf16[192,512,2,128]{3,1,2,0:T(8,128)(2,1)} fusion(bf16[64,512,2,128]{3,1,2,0:T(8,128)(2,1)} %copy.50, s32[1024]{0:T(1024)S(1)} %pad_clamp_fusion), kind=kCustom, calls=%fused_computation.1 | custom fusion | bytes 100664064 | tf_op jit(solution)/shard_map/gather | solution.py:162
  280.0 21.2 %psum.37 = f32[512]{0:T(512)S(1)} all-reduce(f32[512]{0:T(512)S(1)} %fusion.15), channel_id=1, replica_groups=mesh['beam'=8,'mp'=4] {'beam'}, use_global_device_ids=true, to_apply=%region_5.0 | all-reduce | flops 512 | bytes 4096 | tf_op jit(solution)/shard_map/psum | solution.py:108
  301.2 1.3 broadcast_multiply_fusion
  303.0 2.5 multiply_bitcast_fusion
  305.6 0.9 copy.55
  306.5 1.4 subtract_convert_fusion
  307.9 1.2 pad_maximum_fusion
  309.6 0.7 convolution_convert_fusion
  311.2 22.1 %multiply_reduce_fusion = (f32[192,2,8]{2,1,0:T(2,128)S(1)}, f32[192,2,8,512]{3,2,1,0:T(8,128)}) fusion(bf16[192,2,8,128]{3,2,1,0:T(8,128)(2,1)S(1)} %bitcast.68, bf16[192,512,2,128]{3,1,2,0:T(8,128)(2,1)} %gather_fusion), kind=kOutput, calls=%fused_computation.8 | convolution fusion | flops 405795840 | bytes 57421824 | tf_op jit(solution)/shard_map/bkgd,blkd->bkgl/dot_general | solution.py:54
  333.7 3.8 fusion.4
  338.0 20.1 %add_convert_fusion.1 = bf16[192,2,8,128]{3,2,1,0:T(8,128)(2,1)S(1)} fusion(bf16[192,512,2,128]{3,1,2,0:T(8,128)(2,1)} %gather_fusion.1, f32[192,2,8,512]{3,2,1,0:T(8,128)} %get-tuple-element.19, f32[192,2,8]{2,1,0:T(2,128)S(1)} %copy.48, f32[192,2,8]{2,1,0:T(2,128)S(1)} %copy.46, f32[192,2,128]{2,1,0:T(2,128)S(1)} %reshape.154, f32[192,2,8]{2,1,0:T(2,128)S(1)} %copy.51), kind=kOutput, calls=%fused_computation.30 | convolution fusion | flops 410124288 | bytes 57643008 | tf_op jit(solution)/shard_map/bkgl,blkd->bkgd/dot_general | solution.py:67
  358.1 2.1 convolution_convert_fusion.1
  360.3 224.5 %all-gather.3.cloned.1.call-done = bf16[4096,2048]{1,0:T(8,128)(2,1)} async-done(((bf16[512,2048]{1,0:T(8,128)(2,1)}), bf16[4096,2048]{1,0:T(8,128)(2,1)}) %all-gather.3.cloned.1.call-update) | async-done | bytes 16777232 | tf_op jit(solution)/shard_map/all_gather | solution.py:14
  584.8 9.5 %reduce_sum.45 = bf16[512,2048]{1,0:T(8,128)(2,1)S(1)} reduce(bf16[8,512,2048]{2,1,0:T(8,128)(2,1)} %bitcast.65, bf16[]{:T(256)} %constant.80.clone.1), dimensions={0}, to_apply=%region_11.12 | reduce | flops 7340032 | bytes 18874370 | tf_op jit(solution)/shard_map/reduce_sum | solution.py:14
  594.2 5.9 fusion.44
  600.2 0.6 constant_dynamic-slice_fusion.1
  601.4 28.2 %reduce-scatter.2.cloned.1.call-done = f32[128,1024]{1,0:T(8,128)} async-done(((f32[512,1024]{1,0:T(8,128)}), f32[128,1024]{1,0:T(8,128)}) %reduce-scatter.2.cloned.1.call-update) | async-done | bytes 524304 | tf_op jit(solution)/shard_map/reduce_scatter | solution.py:182
  629.7 1.8 convert_element_type.113
  (61 shorter events, 5.1 us)
Async XLA Ops:
  7.2 98.3 %copy-start = (bf16[1024,256]{1,0:T(8,128)(2,1)S(1)}, bf16[1024,256]{1,0:T(8,128)(2,1)}, u32[]{:S(2)}) copy-start(bf16[1024,256]{1,0:T(8,128)(2,1)} %param.16) | copy-start | bytes 1572868
  7.2 91.4 %all-reduce.5.cloned.1.call-start = ((), (), s32[]{:S(2)}) async-start(), calls=%async_computation.1 | async-start | bytes 2097152 | tf_op jit(solution)/shard_map/psum | solution.py:99
  23.2 40.8 %copy-start.4 = (bf16[1024]{0:T(1024)(128)(2,1)S(1)}, bf16[1024]{0:T(1024)(128)(2,1)}, u32[]{:S(2)}) copy-start(bf16[1024]{0:T(1024)(128)(2,1)} %param.13) | copy-start | bytes 6148
  63.9 237.3 %all-reduce.7.cloned.1.call-start = ((), (), s32[]{:S(2)}) async-start(), calls=%async_computation.4 | async-start | bytes 10485760 | tf_op jit(solution)/shard_map/psum | solution.py:108
  64.0 42.7 %copy-start.5 = (bf16[1024,256]{1,0:T(8,128)(2,1)S(1)}, bf16[1024,256]{1,0:T(8,128)(2,1)}, u32[]{:S(2)}) copy-start(bf16[1024,256]{1,0:T(8,128)(2,1)} %param.15) | copy-start | bytes 1572868
  98.6 6.9 %copy-start.2 = (bf16[512,1024]{1,0:T(8,128)(2,1)S(1)}, bf16[512,1024]{1,0:T(8,128)(2,1)}, u32[]{:S(2)}) copy-start(bf16[512,1024]{1,0:T(8,128)(2,1)} %all-reduce.5.cloned.1.call-done) | copy-start | bytes 3145732
  106.7 1.4 copy-start.3
  108.0 476.8 %all-gather.3.cloned.1.call-start = ((), (), s32[]{:S(2)}) async-start(), calls=%async_computation.3 | async-start | bytes 18874368 | tf_op jit(solution)/shard_map/all_gather | solution.py:14
  360.3 269.4 %reduce-scatter.2.cloned.1.call-start = ((), (), s32[]{:S(2)}) async-start(), calls=%async_computation.2 | async-start | bytes 2621440 | tf_op jit(solution)/shard_map/reduce_scatter | solution.py:182
  594.2 37.2 %copy-start.1 = (bf16[1024,256]{1,0:T(8,128)(2,1)S(1)}, bf16[1024,256]{1,0:T(8,128)(2,1)}, u32[]{:S(2)}) copy-start(bf16[1024,256]{1,0:T(8,128)(2,1)} %param.16) | copy-start | bytes 1572868
Sparse Core Ops, SparseCore 0:
  64.0 34.4 all-reduce.4
  108.1 184.6 all-reduce.6
  360.4 224.3 all-gather.2
  600.3 29.3 reduce-scatter.1
